TPU v7x, 32 devices: a whole 2x2x4 slice. The times are simulated.
32 devices in a mesh: groups: 2 (over y), sec: 4 (over z), blk: 4 (over x, core).
Axes of the slice: x: 2, y: 2, z: 4, core: 2. Of those that a mesh axis runs over, the one named last changes fastest.
Arguments:
- psi: bfloat16 [8, 4, 256, 256], P(('groups', 'sec'), 'blk'), parts along dimension 0, may hold values from -6 to 6
- own_env: bfloat16 [8, 4, 17, 256, 256], P(('groups', 'sec'), 'blk'), parts along dimension 0, may hold values from -0.375 to 0.375
- handoff_env: bfloat16 [8, 4, 17, 256, 256], P(('groups', 'sec'), 'blk'), parts along dimension 0, may hold values from -0.375 to 0.375
- sources: int32 [8, 4, 17], P(('groups', 'sec'), 'blk'), parts along dimension 0, may hold values from 0 to 3, as said below
Outputs:
- applied: bfloat16 [8, 4, 256, 256], P(('groups', 'sec'), 'blk'), parts along dimension 0
- rayleigh: float32 [8], P(('groups', 'sec')), parts along dimension 0
- residual_scale: float32 [8], P(('groups', 'sec')), parts along dimension 0
There are 2 independent parts, one for each index of `groups`. A program takes and returns all parts, laid end to end along the dimension named above; each array names one. Nothing has to cross between parts.
Inputs may be any that keep to these rules, and one draw needn't show every extreme that they name: `sources`: every entry names a sector of the same section, and the 17 channels of each output sector name every one of the 4 sectors of its section.
All inputs are finite; a program needn't handle non-finite values.
Results may differ from a plain program's by a relative error of at most 0.0064.
Values may be sent and summed in bfloat16 or wider, within the bound.
No kernel may reach another device: no remote copies, remote signals or barrier semaphores. Data moves between devices by JAX's collectives and lax.ppermute only.
A program may use at most 64 MiB of HBM per device.

v0:
```python
import jax
import jax.numpy as jnp
from jax import lax
from jax.sharding import PartitionSpec as P


def from_partner(value, axis, apart):
    return lax.ppermute(value, axis, [(i, i ^ 1 << apart) for i in range(lax.axis_size(axis))])


def contract(picked, left, right):
    inner = jnp.einsum("qcab,qcbd->qcad", picked, right, preferred_element_type=jnp.float32).astype(
        jnp.bfloat16
    )
    return jnp.einsum("qcab,qcbd->qad", left, inner, preferred_element_type=jnp.float32)


def shards(psi, own_env, handoff_env, sources):
    partner = from_partner(handoff_env, "sec", 0)
    even = lax.axis_index("sec") % 2 == 0
    left = jnp.where(even, own_env[0], partner[0])
    right = jnp.where(even, partner[0], own_env[0])
    sec_dev = psi.shape[1]
    channels = sources.shape[2]
    block = psi.shape[2]
    width = lax.axis_size("blk")
    own_list = sources[0].reshape(-1)
    vector = psi[0]
    whole_psi = lax.all_gather(vector, "blk", axis=0, tiled=True)
    picked = whole_psi[own_list].reshape(sec_dev, channels, block, block)
    first = contract(picked, left, right)
    widened = vector.astype(jnp.float32)
    count = width * sec_dev * block * block
    along, mass, squared = lax.psum(
        (jnp.sum(widened * first), jnp.sum(widened * widened), jnp.sum(first * first)), "blk"
    )
    alpha = along / mass
    resid = first - alpha * widened
    power = squared - alpha * along
    scale = jnp.sqrt(power / count + 1e-06)
    second = (resid / scale).astype(jnp.bfloat16)
    whole_second = lax.all_gather(second, "blk", axis=0, tiled=True)
    repicked = whole_second[own_list].reshape(sec_dev, channels, block, block)
    applied = contract(repicked, left, right).astype(jnp.bfloat16)
    return (applied[None], alpha.reshape(1), scale.reshape(1))


def solution(mesh):
    in_specs = (
        P(("groups", "sec"), "blk", None, None),
        P(("groups", "sec"), "blk", None, None, None),
        P(("groups", "sec"), "blk", None, None, None),
        P(("groups", "sec"), "blk", None),
    )
    out_specs = (
        P(("groups", "sec"), "blk", None, None),
        P(("groups", "sec")),
        P(("groups", "sec")),
    )
    return jax.shard_map(shards, mesh=mesh, in_specs=in_specs, out_specs=out_specs, check_vma=False)
```

profile of v0, /device:TPU:0, one launch (start us, length us, event | category | flops | bytes accessed | tf_op | source)
XLA Modules:
  0.0 80.9 jit_solution(6384535929502615253)
XLA Ops:
  0.6 3.1 %collective-permute-start = (bf16[1,1,17,256,256]{4,3,2,1,0:T(8,128)(2,1)}, bf16[1,1,17,256,256]{4,3,2,1,0:T(8,128)(2,1)}, u32[]{:S(2)}, u32[]{:S(2)}) collective-permute-start(bf16[1,1,17,256,256]{4,3,2,1,0:T(8,128)(2,1)} %param.6), channel_id=1, source_target_pairs={{0,4},{4,0},{8,12},{12,8},{1,5},{5,1},{9,13},{13,9},{2,6},{6,2},{1... | collective-permute-start | bytes 6684680 | tf_op jit(solution)/shard_map/ppermute | solution.py:8
  3.7 0.7 fusion.53
  4.4 7.4 %all-gather = bf16[4,1,256,256]{3,2,1,0:T(8,128)(2,1)S(1)} all-gather(bf16[1,1,256,256]{3,2,1,0:T(8,128)(2,1)} %param.4), channel_id=2, replica_groups=mesh['groups'=2,'sec'=4,'blk'=4] {'blk'}, dimensions={0}, use_global_device_ids=true | all-gather | bytes 655360 | tf_op jit(solution)/shard_map/all_gather | solution.py:29
  11.8 0.0 copy-start
  11.8 0.7 gather_fusion
  12.5 0.2 copy-done
  12.7 0.7 fusion.52
  13.4 39.1 %collective-permute-done = bf16[1,1,17,256,256]{4,3,2,1,0:T(8,128)(2,1)} collective-permute-done((bf16[1,1,17,256,256]{4,3,2,1,0:T(8,128)(2,1)}, bf16[1,1,17,256,256]{4,3,2,1,0:T(8,128)(2,1)}, u32[]{:S(2)}, u32[]{:S(2)}) %collective-permute-start) | collective-permute-done | bytes 2228256 | tf_op jit(solution)/shard_map/ppermute | solution.py:8
  52.5 4.4 %fusion.48 = (f32[]{:T(128)}, f32[]{:T(128)}, f32[256,256]{1,0:T(8,128)S(1)}) fusion(bf16[1,1,256,256]{3,2,1,0:T(8,128)(2,1)S(1)} %copy-done, bf16[17,256,256]{2,1,0:T(8,128)(2,1)S(1)} %gather_fusion, bf16[1,1,17,256,256]{4,3,2,1,0:T(8,128)(2,1)} %collective-permute-done, bf16[1,1,17,256,256]{4,3,2,1,0:T(8,128)(2,1)} %param.5, pred[]{:T(512)S(6)} %eq.5), kind=kOutput, calls=%fused_computation.22 | convolution fusion | flops 1144520704 | bytes 7077897 | tf_op jit(solution)/shard_map/qcab,qcbd->qad/dot_general | solution.py:15
  56.9 6.6 %all-reduce = (f32[]{:T(128)}, f32[]{:T(128)}, f32[]{:T(128)}) all-reduce(f32[]{:T(128)} %get-tuple-element.4, f32[]{:T(128)} %get-tuple-element.3, f32[]{:T(128)} %fusion.52), channel_id=1, replica_groups=mesh['groups'=2,'sec'=4,'blk'=4] {'blk'}, use_global_device_ids=true, to_apply=%region_5.6 | all-reduce | flops 3 | bytes 24 | tf_op jit(solution)/shard_map/psum | solution.py:34
  66.2 7.2 %all-gather.1 = bf16[1024,256]{1,0:T(8,128)(2,1)S(1)} all-gather(bf16[256,256]{1,0:T(8,128)(2,1)S(1)} %fusion.51), channel_id=3, replica_groups=mesh['groups'=2,'sec'=4,'blk'=4] {'blk'}, dimensions={0}, use_global_device_ids=true | all-gather | bytes 655360 | tf_op jit(solution)/shard_map/all_gather | solution.py:42
  73.5 0.7 gather_fusion.1
  74.2 4.5 %fusion.39 = bf16[1,1,256,256]{3,2,1,0:T(8,128)(2,1)} fusion(bf16[17,256,256]{2,1,0:T(8,128)(2,1)S(1)} %gather_fusion.1, bf16[1,1,17,256,256]{4,3,2,1,0:T(8,128)(2,1)} %param.5, bf16[1,1,17,256,256]{4,3,2,1,0:T(8,128)(2,1)} %collective-permute-done, pred[]{:T(512)S(6)} %eq.5), kind=kOutput, calls=%fused_computation.17 | convolution fusion | flops 1144258560 | bytes 6815745 | tf_op jit(solution)/shard_map/qcab,qcbd->qad/dot_general | solution.py:15
  (2 shorter events, 0.1 us)
Async XLA Ops:
  0.6 51.9 %collective-permute-start = (bf16[1,1,17,256,256]{4,3,2,1,0:T(8,128)(2,1)}, bf16[1,1,17,256,256]{4,3,2,1,0:T(8,128)(2,1)}, u32[]{:S(2)}, u32[]{:S(2)}) collective-permute-start(bf16[1,1,17,256,256]{4,3,2,1,0:T(8,128)(2,1)} %param.6), channel_id=1, source_target_pairs={{0,4},{4,0},{8,12},{12,8},{1,5},{5,1},{9,13},{13,9},{2,6},{6,2},{1... | collective-permute-start | bytes 6684680 | tf_op jit(solution)/shard_map/ppermute | solution.py:8
  11.8 0.9 %copy-start = (bf16[1,1,256,256]{3,2,1,0:T(8,128)(2,1)S(1)}, bf16[1,1,256,256]{3,2,1,0:T(8,128)(2,1)}, u32[]{:S(2)}) copy-start(bf16[1,1,256,256]{3,2,1,0:T(8,128)(2,1)} %param.4) | copy-start | bytes 393220
where the time goes:
time: 81.1 us; the launch traced here: 80.9 us
  waiting for transfers between devices  39.1 us (48%)
  blocking collectives  21.1 us (26%)
  matrix products  8.91 us (11%)
  between operations  5.62 us (7%)
  starting transfers between devices  3.12 us (4%)
  local copies, waits for them, and re-layouts  1.58 us (2%)
  other arithmetic  1.38 us (2%)
    ppermute x1, waiting for transfers between devices, from_partner(): lax.ppermute(value, axis, [(i, i ^ 1 << apart) for i in range(lax.axis_si...  39.1 us
    dot_general x2, matrix products, contract(): jnp.einsum('qcab,qcbd->qad', left, inner, preferred_element_type=jnp.floa...  8.91 us
    all_gather x1, blocking collectives, shards(): whole_psi = lax.all_gather(vector, 'blk', axis=0, tiled=True)  7.37 us
    all_gather x1, blocking collectives, shards(): whole_second = lax.all_gather(second, 'blk', axis=0, tiled=True)  7.21 us
    psum x1, blocking collectives, shards(): lax.psum((jnp.sum(widened * first), jnp.sum(widened * widened), jnp.sum(f...  6.56 us
    ppermute x1, starting transfers between devices, from_partner(): lax.ppermute(value, axis, [(i, i ^ 1 << apart) for i in range(lax.axis_si...  3.12 us
  transfers between devices with their start and end apart: 1, of which 1 were waited for; matrix products, arithmetic and copies ran while one was open for 2% of the time, Pallas kernels for 0%

commit v1 on v0

v1 whole, which is shorter than its diff:
```python
import functools

import jax
import jax.numpy as jnp
from jax import lax
from jax.experimental import pallas as pl
from jax.experimental.pallas import tpu as pltpu
from jax.sharding import PartitionSpec as P

f32 = jnp.float32
bf16 = jnp.bfloat16
EXTRA = 16


def swap(value, axis, bit):
    return lax.ppermute(value, axis, [(i, i ^ bit) for i in range(lax.axis_size(axis))])


def dot(a, b):
    return jnp.dot(a, b, preferred_element_type=f32)


def stage_kernel(channels, psi, own, env, mass, sem):
    copies = [pltpu.make_async_copy(own.at[c], env.at[c], sem.at[c]) for c in range(channels)]
    for copy in copies:
        copy.start()
    for s in range(psi.shape[0]):
        wide = psi[s].astype(f32)
        total = jnp.sum(wide * wide, axis=(0, 1), keepdims=True)
        mass[s] = jnp.broadcast_to(total, mass.shape[1:])
    for copy in copies:
        copy.wait()


def first_kernel(channels, table, psi, own, partner, mass, env, parts, packed, sem):
    even = table[0] == 0
    me = table[1]
    copies = [pltpu.make_async_copy(partner.at[c], env.at[c], sem.at[c]) for c in range(channels)]
    for copy in copies:
        copy.start()
    parts[...] = jnp.zeros_like(parts)

    def body(left, right):
        for c in range(channels):
            source = table[2 + c]
            copies[c].wait()
            inner = dot(psi[source], right[c]).astype(bf16)
            parts[source] += dot(left[c], inner)

    @pl.when(even)
    def _():
        body(own, env)

    @pl.when(jnp.logical_not(even))
    def _():
        body(env, own)

    first = parts[0]
    for s in range(1, parts.shape[0]):
        first = first + parts[s]
    wide = psi[me].astype(f32)
    along = jnp.sum(wide * first, axis=(0, 1), keepdims=True)
    weight = mass[me][:1, :1]
    share = jnp.where(weight > 0, along / jnp.where(weight > 0, weight, 1.0), 0.0)
    rows = first.shape[0]
    packed[:rows] = (first - share * wide).astype(bf16)
    high = share.astype(bf16).astype(f32)
    middle = (share - high).astype(bf16).astype(f32)
    low = share - high - middle
    row = lax.broadcasted_iota(jnp.int32, (EXTRA, first.shape[1]), 0)
    tail = jnp.where(row == 0, high, jnp.where(row == 1, middle, jnp.where(row == 2, low, 0.0)))
    packed[rows:] = tail.astype(bf16)


def second_kernel(channels, table, vector, psi, own, env, mass, parts, applied, alpha_out, scale_out, total_ref):
    even = table[0] == 0
    width, rows, columns = parts.shape

    share, weight = [], []
    for m in range(width):
        bits = vector[m, rows:].astype(f32)
        share.append(bits[0:1, 0:1] + bits[1:2, 0:1] + bits[2:3, 0:1])
        weight.append(mass[m][:1, :1])
    along = share[0] * weight[0]
    whole = weight[0]
    for m in range(1, width):
        along += share[m] * weight[m]
        whole += weight[m]
    alpha = along / whole

    power = jnp.zeros((1, 1), f32)
    total = jnp.zeros((rows, columns), f32)
    for m in range(width):
        delta = share[m] - alpha
        resid = vector[m, :rows].astype(f32) + delta * psi[m].astype(f32)
        power += jnp.sum(resid * resid, axis=(0, 1), keepdims=True)
        total += delta * parts[m]
    scale = jnp.sqrt(power / (width * rows * columns) + 1e-06)
    total_ref[...] = total

    def body(left, right):
        summed = total_ref[...]
        for c in range(channels):
            summed += dot(left[c], dot(vector[table[2 + c], :rows], right[c]).astype(bf16))
        applied[...] = (summed / scale).astype(bf16)

    @pl.when(even)
    def _():
        body(own, env)

    @pl.when(jnp.logical_not(even))
    def _():
        body(env, own)

    alpha_out[0] = alpha[0, 0]
    scale_out[0] = scale[0, 0]


ANY = pl.BlockSpec(memory_space=pl.ANY)
VMEM = pl.BlockSpec(memory_space=pltpu.VMEM)
SMEM = pl.BlockSpec(memory_space=pltpu.SMEM)
PARAMS = pltpu.CompilerParams(vmem_limit_bytes=24 * 1024 * 1024)


def shards(psi, own_env, handoff_env, sources):
    partner = swap(handoff_env, "sec", 1)[0, 0]
    own = own_env[0, 0]
    channels, block = own.shape[0], own.shape[1:]
    width = lax.axis_size("blk")
    table = jnp.concatenate(
        [jnp.stack([lax.axis_index("sec") % 2, lax.axis_index("blk")]).astype(jnp.int32), sources[0, 0]]
    )
    psis = lax.all_gather(psi[0, 0], "blk", axis=0)
    envs = (channels,) + block
    held, mass = pl.pallas_call(
        functools.partial(stage_kernel, channels),
        in_specs=[VMEM, ANY],
        out_specs=[VMEM, VMEM],
        out_shape=[pltpu.VMEM(envs, bf16), pltpu.VMEM((width, 8, 128), f32)],
        scratch_shapes=[pltpu.SemaphoreType.DMA((channels,))],
        compiler_params=PARAMS,
        name="stage",
    )(psis, own)
    partner_held, parts, packed = pl.pallas_call(
        functools.partial(first_kernel, channels),
        in_specs=[SMEM, VMEM, VMEM, ANY, VMEM],
        out_specs=[VMEM, VMEM, VMEM],
        out_shape=[
            pltpu.VMEM(envs, bf16),
            pltpu.VMEM((width,) + block, f32),
            jax.ShapeDtypeStruct((block[0] + EXTRA, block[1]), bf16),
        ],
        scratch_shapes=[pltpu.SemaphoreType.DMA((channels,))],
        compiler_params=PARAMS,
        name="first",
    )(table, psis, held, partner, mass)
    vectors = lax.all_gather(packed, "blk", axis=0)
    applied, alpha, scale = pl.pallas_call(
        functools.partial(second_kernel, channels),
        in_specs=[SMEM, VMEM, VMEM, VMEM, VMEM, VMEM, VMEM],
        out_specs=[VMEM, SMEM, SMEM],
        out_shape=[
            jax.ShapeDtypeStruct(block, bf16),
            jax.ShapeDtypeStruct((1,), f32),
            jax.ShapeDtypeStruct((1,), f32),
        ],
        scratch_shapes=[pltpu.VMEM(block, f32)],
        compiler_params=PARAMS,
        name="second",
    )(table, vectors, psis, held, partner_held, mass, parts)
    return applied[None, None], alpha, scale


def solution(mesh):
    spec = P(("groups", "sec"), "blk")
    return jax.shard_map(
        shards,
        mesh=mesh,
        in_specs=(spec, spec, spec, spec),
        out_specs=(spec, P(("groups", "sec")), P(("groups", "sec"))),
        check_vma=False,
    )
```

time: 81.1 us -> 74.3 us (0.916)
  Pallas kernels: 0 us -> 17.5 us
  matrix products: 8.91 us -> 0 us
  blocking collectives: 21.1 us -> 14.9 us
  between operations: 5.62 us -> 0.67 us
  waiting for transfers between devices: 39.1 us -> 36.3 us
  other arithmetic: 1.38 us -> 0.08 us
    pallas_call x0 -> x3, Pallas kernels: none -> 17.5 us  [the longest x1 10.7 us: shards(): pl.pallas_call(functools.partial(first_kernel, channels), in_specs=[SMEM,...]
    dot_general x2 -> x0, matrix products: 8.91 us -> none  [contract(): jnp.einsum('qcab,qcbd->qad', left, inner, preferred_element_type=jnp.floa...]
    psum x1 -> x0, blocking collectives: 6.56 us -> none  [shards(): lax.psum((jnp.sum(widened * first), jnp.sum(widened * widened), jnp.sum(f...]
    ppermute x1, waiting for transfers between devices: 39.1 us -> 36.3 us  [swap(): lax.ppermute(value, axis, [(i, i ^ bit) for i in range(lax.axis_size(axis...]
    unnamed x2 -> x4, local copies, waits for them, and re-layouts: 0.21 us -> 1.63 us
    gather x2 -> x0, local copies, waits for them, and re-layouts: 1.38 us -> none  [the longest x1 0.69 us: shards(): picked = whole_psi[own_list].reshape(sec_dev, channels, block, block)]
  transfers between devices with their start and end apart: 1 -> 1, of which waited for: 1 -> 1; matrix products, arithmetic and copies ran while one was open for 2% -> 0% of each run, Pallas kernels for 0% -> 4%
where the time goes in v1:
time: 74.3 us; the launch traced here: 74.2 us
  waiting for transfers between devices  36.3 us (49%)
  Pallas kernels  17.5 us (24%)
  blocking collectives  14.9 us (20%)
  starting transfers between devices  3.12 us (4%)
  local copies, waits for them, and re-layouts  1.63 us (2%)
    ppermute x1, waiting for transfers between devices, swap(): lax.ppermute(value, axis, [(i, i ^ bit) for i in range(lax.axis_size(axis...  36.3 us
    pallas_call x1, Pallas kernels, shards(): pl.pallas_call(functools.partial(first_kernel, channels), in_specs=[SMEM,...  10.7 us
    all_gather x1, blocking collectives, shards(): vectors = lax.all_gather(packed, 'blk', axis=0)  7.51 us
    all_gather x1, blocking collectives, shards(): psis = lax.all_gather(psi[0, 0], 'blk', axis=0)  7.37 us
    pallas_call x1, Pallas kernels, shards(): pl.pallas_call(functools.partial(second_kernel, channels), in_specs=[SMEM...  3.52 us
    pallas_call x1, Pallas kernels, shards(): pl.pallas_call(functools.partial(stage_kernel, channels), in_specs=[VMEM,...  3.26 us
    ppermute x1, starting transfers between devices, swap(): lax.ppermute(value, axis, [(i, i ^ bit) for i in range(lax.axis_size(axis...  3.12 us
    unnamed x4, local copies, waits for them, and re-layouts  1.63 us
  transfers between devices with their start and end apart: 1, of which 1 were waited for; matrix products, arithmetic and copies ran while one was open for 0% of the time, Pallas kernels for 4%

profile of v1, /device:TPU:0, one launch (start us, length us, event | category | flops | bytes accessed | tf_op | source)
XLA Modules:
  0.0 74.2 jit_solution(14620847888392130967)
XLA Ops:
  0.6 0.0 copy-start.1
  0.6 3.1 %collective-permute-start = (bf16[1,1,17,256,256]{4,3,2,1,0:T(8,128)(2,1)}, bf16[1,1,17,256,256]{4,3,2,1,0:T(8,128)(2,1)S(1)}, u32[]{:S(2)}, u32[]{:S(2)}) collective-permute-start(bf16[1,1,17,256,256]{4,3,2,1,0:T(8,128)(2,1)} %param.6), channel_id=1, source_target_pairs={{0,4},{4,0},{8,12},{12,8},{1,5},{5,1},{9,13},{13,9},{2,6},{6,2},{1... | collective-permute-start | bytes 6684680 | tf_op jit(solution)/shard_map/ppermute | solution.py:16
  3.8 7.4 %all-gather = bf16[4,1,256,256]{3,2,1,0:T(8,128)(2,1)S(1)} all-gather(bf16[1,1,256,256]{3,2,1,0:T(8,128)(2,1)} %param.4), channel_id=2, replica_groups=mesh['groups'=2,'sec'=4,'blk'=4] {'blk'}, dimensions={0}, use_global_device_ids=true | all-gather | bytes 655360 | tf_op jit(solution)/shard_map/all_gather | solution.py:133
  11.1 0.0 copy-start
  11.1 1.6 %copy-done = bf16[1,1,17,256,256]{4,3,2,1,0:T(8,128)(2,1)S(1)} copy-done((bf16[1,1,17,256,256]{4,3,2,1,0:T(8,128)(2,1)S(1)}, bf16[1,1,17,256,256]{4,3,2,1,0:T(8,128)(2,1)}, u32[]{:S(2)}) %copy-start) | copy-done | bytes 2228248
  12.8 3.3 %stage.1 = (bf16[17,256,256]{2,1,0:T(8,128)(2,1)S(1)}, f32[4,8,128]{2,1,0:T(8,128)S(1)}) custom-call(bf16[4,256,256]{2,1,0:T(8,128)(2,1)S(1)} %bitcast.8, bf16[17,256,256]{2,1,0:T(8,128)(2,1)S(1)} %bitcast.12), custom_call_target="tpu_custom_call" | custom-call | tf_op jit(solution)/shard_map/stage/pallas_call | solution.py:135
  16.0 0.0 copy-done.1
  16.0 0.1 pad_add_fusion.table
  16.1 36.3 %collective-permute-done = bf16[1,1,17,256,256]{4,3,2,1,0:T(8,128)(2,1)S(1)} collective-permute-done((bf16[1,1,17,256,256]{4,3,2,1,0:T(8,128)(2,1)}, bf16[1,1,17,256,256]{4,3,2,1,0:T(8,128)(2,1)S(1)}, u32[]{:S(2)}, u32[]{:S(2)}) %collective-permute-start) | collective-permute-done | bytes 2228256 | tf_op jit(solution)/shard_map/ppermute | solution.py:16
  52.4 10.7 %first.1 = (bf16[17,256,256]{2,1,0:T(8,128)(2,1)S(1)}, f32[4,256,256]{2,1,0:T(8,128)S(1)}, bf16[272,256]{1,0:T(8,128)(2,1)S(1)}) custom-call(s32[19]{0:T(128)S(1)} %pad_add_fusion.table, bf16[4,256,256]{2,1,0:T(8,128)(2,1)S(1)} %bitcast.9, bf16[17,256,256]{2,1,0:T(8,128)(2,1)S(1)} %get-tuple-element.11.own, bf16[17,256,256]{2,1,0:T(8,128)(2,1)S(1)} %bitcast.11, ...), custom_call_target="tpu_custom_call" | custom-call | tf_op jit(solution)/shard_map/first/pallas_call | solution.py:144
  63.1 7.5 %all-gather.1 = bf16[1088,256]{1,0:T(8,128)(2,1)S(1)} all-gather(bf16[272,256]{1,0:T(8,128)(2,1)S(1)} %get-tuple-element.13), channel_id=3, replica_groups=mesh['groups'=2,'sec'=4,'blk'=4] {'blk'}, dimensions={0}, use_global_device_ids=true | all-gather | bytes 696320 | tf_op jit(solution)/shard_map/all_gather | solution.py:157
  70.7 3.5 %second.1 = (bf16[256,256]{1,0:T(8,128)(2,1)}, f32[1]{0:T(128)}, f32[1]{0:T(128)}) custom-call(s32[19]{0:T(128)S(1)} %pad_add_fusion.table, bf16[4,272,256]{2,1,0:T(8,128)(2,1)S(1)} %bitcast.13, bf16[4,256,256]{2,1,0:T(8,128)(2,1)S(1)} %bitcast.10, bf16[17,256,256]{2,1,0:T(8,128)(2,1)S(1)} %get-tuple-element.11.own, ...), custom_call_target="tpu_custom_call" | custom-call | tf_op jit(solution)/shard_map/second/pallas_call | solution.py:158
Async XLA Ops:
  0.6 15.4 %copy-start.1 = (s32[1,1,17]{2,1,0:T(1,128)S(1)}, s32[1,1,17]{2,1,0:T(1,128)}, u32[]{:S(2)}) copy-start(s32[1,1,17]{2,1,0:T(1,128)} %param.7) | copy-start | bytes 208
  0.6 51.8 %collective-permute-start = (bf16[1,1,17,256,256]{4,3,2,1,0:T(8,128)(2,1)}, bf16[1,1,17,256,256]{4,3,2,1,0:T(8,128)(2,1)S(1)}, u32[]{:S(2)}, u32[]{:S(2)}) collective-permute-start(bf16[1,1,17,256,256]{4,3,2,1,0:T(8,128)(2,1)} %param.6), channel_id=1, source_target_pairs={{0,4},{4,0},{8,12},{12,8},{1,5},{5,1},{9,13},{13,9},{2,6},{6,2},{1... | collective-permute-start | bytes 6684680 | tf_op jit(solution)/shard_map/ppermute | solution.py:16
  11.1 1.6 %copy-start = (bf16[1,1,17,256,256]{4,3,2,1,0:T(8,128)(2,1)S(1)}, bf16[1,1,17,256,256]{4,3,2,1,0:T(8,128)(2,1)}, u32[]{:S(2)}) copy-start(bf16[1,1,17,256,256]{4,3,2,1,0:T(8,128)(2,1)} %param.5) | copy-start | bytes 6684676

commit v2 on v0

v2 whole, which is shorter than its diff:
```python
import functools

import jax
import jax.numpy as jnp
from jax import lax
from jax.experimental import pallas as pl
from jax.experimental.pallas import tpu as pltpu
from jax.sharding import PartitionSpec as P


f32 = jnp.float32
bf16 = jnp.bfloat16
EXTRA = 16
GROUP = 5

ANY = pl.BlockSpec(memory_space=pl.ANY)
HBM = pl.BlockSpec(memory_space=pltpu.HBM)
VMEM = pl.BlockSpec(memory_space=pltpu.VMEM)
SMEM = pl.BlockSpec(memory_space=pltpu.SMEM)
PARAMS = pltpu.CompilerParams(vmem_limit_bytes=16 * 1024 * 1024)


def swap(value, axis, bit):
    return lax.ppermute(value, axis, [(i, i ^ bit) for i in range(lax.axis_size(axis))])


def dot(a, b):
    return jnp.dot(a, b, preferred_element_type=f32)


def total_of(x):
    return jnp.sum(x, axis=(0, 1), keepdims=True)


def call(kernel, ins, outs, args, flops, aliases=None, scratch=()):
    return pl.pallas_call(
        kernel,
        in_specs=ins,
        out_specs=[spec for spec, _ in outs],
        out_shape=[shape for _, shape in outs],
        scratch_shapes=scratch,
        input_output_aliases=aliases or {},
        compiler_params=PARAMS,
        cost_estimate=pl.CostEstimate(flops=flops, transcendentals=0, bytes_accessed=0),
    )(*args)


def one_channel(table, psi, env, c):
    parity = table[0]
    source = table[2 + c]
    inner = dot(psi[source], env[1 - parity, c]).astype(bf16)
    return source, dot(env[parity, c], inner)


def opening_kernel(table, psi, own, chunk, env, parts, mass, order, starts, sem):
    copy = pltpu.make_async_copy(own, env.at[0], sem)
    copy.start()
    channels = own.shape[0]
    width = psi.shape[0]
    me = table[1]
    for k in range(chunk.shape[0]):
        env[1, k] = chunk[k]
    parts[...] = jnp.zeros_like(parts)
    for s in range(width):
        wide = psi[s].astype(f32)
        mass[s] = jnp.broadcast_to(total_of(wide * wide), mass.shape[1:])

    def by_source(m, place):
        starts[m] = place

        def look(c, at):
            order[at] = c
            return at + (table[2 + c] ^ me == m).astype(jnp.int32)

        return lax.fori_loop(0, channels, look, place)

    starts[width] = lax.fori_loop(0, width, by_source, 0)
    copy.wait()
    for k in range(chunk.shape[0]):
        source, product = one_channel(table, psi, env, k)
        parts[source] += product


def middle_kernel(base, table, psi, chunk, env_in, parts_in, env, parts, early, along):
    for k in range(chunk.shape[0]):
        env[1, base + k] = chunk[k]
    for k in range(chunk.shape[0]):
        source, product = one_channel(table, psi, env, base + k)
        parts[source] += product
    total = parts[0]
    for s in range(1, parts.shape[0]):
        total = total + parts[s]
    early[...] = total
    along[...] = jnp.broadcast_to(total_of(psi[table[1]].astype(f32) * total), along.shape)


def closing_kernel(base, table, psi, chunk, env_in, parts_in, early, along, mass, env, parts, packed):
    me = table[1]
    first = early[...]
    for k in range(chunk.shape[0]):
        env[1, base + k] = chunk[k]
    late = None
    for k in range(chunk.shape[0]):
        source, product = one_channel(table, psi, env, base + k)
        parts[source] += product
        late = product if late is None else late + product
    wide = psi[me].astype(f32)
    along_all = along[:1, :1] + total_of(wide * late)
    weight = mass[me][:1, :1]
    share = jnp.where(weight > 0, along_all / jnp.where(weight > 0, weight, 1.0), 0.0)
    rows, columns = first.shape
    packed[:rows] = (first + late - share * wide).astype(bf16)
    high = share.astype(bf16).astype(f32)
    middle = (share - high).astype(bf16).astype(f32)
    low = share - high - middle
    row = lax.broadcasted_iota(jnp.int32, (EXTRA, columns), 0)
    tail = jnp.where(row == 0, high, jnp.where(row == 1, middle, jnp.where(row == 2, low, 0.0)))
    packed[rows:] = tail.astype(bf16)


def second_kernel(low, high, more, width, table, order, starts, psi, env, *refs):
    count = high - low
    blocks, refs = refs[:count], refs[count:]
    if low:
        before, refs = refs[0], refs[1:]
    if high == width:
        (mass, parts), refs = refs[:2], refs[2:]
        stats_in, refs = refs[:more], refs[more:]
        applied, alpha_out, scale_out, summed, held = refs
    else:
        summed, stats, held = refs
    parity, me = table[0], table[1]
    rows, columns = psi.shape[1:]

    for k in range(count):
        held[k] = blocks[k][:rows]

    summed[...] = before[...] if low else jnp.zeros((rows, columns), f32)
    begin, end = starts[low], starts[high]

    def step(g, carry):
        total = None
        for k in range(GROUP):
            place = begin + g * GROUP + k
            valid = place < end
            c = order[jnp.where(valid, place, 0)]
            m = jnp.where(valid, (table[2 + c] ^ me) - low, 0)
            inner = jnp.where(valid, dot(held[m], env[1 - parity, c]), 0.0).astype(bf16)
            product = dot(env[parity, c], inner)
            total = product if total is None else total + product
        summed[...] += total
        return carry

    lax.fori_loop(0, (end - begin + GROUP - 1) // GROUP, step, 0)

    mine = []
    for k in range(count):
        bits = blocks[k][rows:].astype(f32)
        share = bits[0:1, 0:1] + bits[1:2, 0:1] + bits[2:3, 0:1]
        value = held[k].astype(f32)
        cross = total_of(value * psi[me ^ (low + k)].astype(f32))
        mine.append((share, total_of(value * value), cross))
    if high < width:
        for k in range(count):
            for j in range(3):
                stats[k, j] = jnp.broadcast_to(mine[k][j], stats.shape[2:])
        return

    triples = []
    for ref in stats_in:
        for k in range(ref.shape[0]):
            triples.append(tuple(ref[k, j][:1, :1] for j in range(3)))
    triples += mine
    along = jnp.zeros((1, 1), f32)
    whole = jnp.zeros((1, 1), f32)
    for m in range(width):
        weight = mass[me ^ m][:1, :1]
        along += triples[m][0] * weight
        whole += weight
    alpha = along / whole
    power = jnp.zeros((1, 1), f32)
    total = summed[...]
    for m in range(width):
        share, square, cross = triples[m]
        delta = share - alpha
        power += square + 2.0 * delta * cross + delta * delta * mass[me ^ m][:1, :1]
        total += delta * parts[me ^ m]
    scale = jnp.sqrt(power / (width * rows * columns) + 1e-06)
    applied[...] = (total / scale).astype(bf16)
    alpha_out[0] = alpha[0, 0]
    scale_out[0] = scale[0, 0]


def chunk_sizes(channels):
    return [2, channels - 6, 3, 1]


def shards(psi, own_env, handoff_env, sources):
    own, handoff = own_env[0, 0], handoff_env[0, 0]
    channels, block = own.shape[0], own.shape[1:]
    width = lax.axis_size("blk")
    work = 4 * block[0] ** 3
    sizes = chunk_sizes(channels)
    chunks, bases, base = [], [], 0
    for size in sizes:
        chunks.append(swap(handoff[base : base + size], "sec", 1))
        bases.append(base)
        base += size
    table = jnp.concatenate(
        [jnp.stack([lax.axis_index("sec") % 2, lax.axis_index("blk")]).astype(jnp.int32), sources[0, 0]]
    )
    psis = lax.all_gather(psi[0, 0], "blk", axis=0)

    env_shape = (VMEM, pltpu.VMEM((2, channels) + block, bf16))
    parts_shape = (VMEM, pltpu.VMEM((width,) + block, f32))
    tile = (8, 128)
    env, parts, mass, order, starts = call(
        opening_kernel,
        [SMEM, VMEM, HBM, VMEM],
        [
            env_shape,
            parts_shape,
            (VMEM, pltpu.VMEM((width,) + tile, f32)),
            (SMEM, jax.ShapeDtypeStruct((channels + 1,), jnp.int32)),
            (SMEM, jax.ShapeDtypeStruct((width + 1,), jnp.int32)),
        ],
        (table, psis, own, chunks[0]),
        work * sizes[0],
        scratch=[pltpu.SemaphoreType.DMA],
    )
    for k in range(1, len(sizes) - 1):
        env, parts, early, along = call(
            functools.partial(middle_kernel, bases[k]),
            [SMEM, VMEM, VMEM, VMEM, VMEM],
            [env_shape, parts_shape, (VMEM, pltpu.VMEM(block, f32)), (VMEM, pltpu.VMEM(tile, f32))],
            (table, psis, chunks[k], env, parts),
            work * sizes[k],
            aliases={3: 0, 4: 1},
        )
    env, parts, packed = call(
        functools.partial(closing_kernel, bases[-1]),
        [SMEM, VMEM, VMEM, VMEM, VMEM, VMEM, VMEM, VMEM],
        [env_shape, parts_shape, (VMEM, pltpu.VMEM((block[0] + EXTRA, block[1]), bf16))],
        (table, psis, chunks[-1], env, parts, early, along, mass),
        work * sizes[-1],
        aliases={3: 0, 4: 1},
    )

    blocks = {0: packed}
    bit = width // 2
    while bit:
        for m in sorted(blocks):
            blocks[m | bit] = swap(blocks[m], "blk", bit)
        bit //= 2

    cuts = sorted({0, min(2, width - 1), width - 1, width})
    summed, stats = None, []
    for low, high in zip(cuts[:-1], cuts[1:]):
        count = high - low
        last = high == width
        args = [table, order, starts, psis, env] + [blocks[m] for m in range(low, high)]
        specs = [SMEM, SMEM, SMEM, VMEM, VMEM] + [VMEM] * count
        if low:
            args.append(summed)
            specs.append(VMEM)
        scratch = [pltpu.VMEM((count,) + block, bf16)]
        if last:
            args += [mass, parts] + stats
            specs += [VMEM] * (2 + len(stats))
            outs = [
                (VMEM, jax.ShapeDtypeStruct(block, bf16)),
                (SMEM, jax.ShapeDtypeStruct((1,), f32)),
                (SMEM, jax.ShapeDtypeStruct((1,), f32)),
            ]
            scratch = [pltpu.VMEM(block, f32)] + scratch
        else:
            outs = [
                (VMEM, pltpu.VMEM(block, f32)),
                (VMEM, pltpu.VMEM((count, 3) + tile, f32)),
            ]
        result = call(
            functools.partial(second_kernel, low, high, len(stats), width),
            specs,
            outs,
            tuple(args),
            work * channels * count // width,
            scratch=scratch,
        )
        if not last:
            summed = result[0]
            stats.append(result[1])
    applied, alpha, scale = result
    return applied[None, None], alpha, scale


def solution(mesh):
    spec = P(("groups", "sec"), "blk")
    return jax.shard_map(
        shards,
        mesh=mesh,
        in_specs=(spec, spec, spec, spec),
        out_specs=(spec, P(("groups", "sec")), P(("groups", "sec"))),
        check_vma=False,
    )
```

time: 81.1 us -> 67.9 us (0.84)
  Pallas kernels: 0 us -> 14.5 us
  blocking collectives: 21.1 us -> 7.59 us
  matrix products: 8.91 us -> 0 us
  waiting for transfers between devices: 39.1 us -> 30.8 us
  local copies, waits for them, and re-layouts: 1.58 us -> 7.01 us
  between operations: 5.62 us -> 0.72 us
  starting transfers between devices: 3.12 us -> 6.89 us
  other arithmetic: 1.38 us -> 0.08 us
    pallas_call x0 -> x7, Pallas kernels: none -> 14.5 us  [call(): pl.pallas_call(kernel, in_specs=ins, out_specs=[spec for spec, _ in outs]...]
    dot_general x2 -> x0, matrix products: 8.91 us -> none  [contract(): jnp.einsum('qcab,qcbd->qad', left, inner, preferred_element_type=jnp.floa...]
    ppermute x1 -> x7, waiting for transfers between devices: 39.1 us -> 30.8 us  [swap(): lax.ppermute(value, axis, [(i, i ^ bit) for i in range(lax.axis_size(axis...]
    slice x0 -> x4, local copies, waits for them, and re-layouts: none -> 6.99 us  [shards(): chunks.append(swap(handoff[base:base + size], 'sec', 1))]
    all_gather x2 -> x1, blocking collectives: 14.6 us -> 7.59 us  [shards(): psis = lax.all_gather(psi[0, 0], 'blk', axis=0)]
    psum x1 -> x0, blocking collectives: 6.56 us -> none  [shards(): lax.psum((jnp.sum(widened * first), jnp.sum(widened * widened), jnp.sum(f...]
    ppermute x1 -> x7, starting transfers between devices: 3.12 us -> 6.89 us  [swap(): lax.ppermute(value, axis, [(i, i ^ bit) for i in range(lax.axis_size(axis...]
    gather x2 -> x0, local copies, waits for them, and re-layouts: 1.38 us -> none  [the longest x1 0.69 us: shards(): picked = whole_psi[own_list].reshape(sec_dev, channels, block, block)]
  transfers between devices with their start and end apart: 1 -> 7, of which waited for: 1 -> 4; matrix products, arithmetic and copies ran while one was open for 2% -> 6% of each run, Pallas kernels for 0% -> 16%
where the time goes in v2:
time: 67.9 us; the launch traced here: 67.6 us
  waiting for transfers between devices  30.8 us (45%)
  Pallas kernels  14.5 us (21%)
  blocking collectives  7.59 us (11%)
  local copies, waits for them, and re-layouts  7.01 us (10%)
  starting transfers between devices  6.89 us (10%)
  between operations  0.72 us (1%)
    ppermute x7, waiting for transfers between devices, swap(): lax.ppermute(value, axis, [(i, i ^ bit) for i in range(lax.axis_size(axis...  30.8 us
    pallas_call x7, Pallas kernels, call(): pl.pallas_call(kernel, in_specs=ins, out_specs=[spec for spec, _ in outs]...  14.5 us
    all_gather x1, blocking collectives, shards(): psis = lax.all_gather(psi[0, 0], 'blk', axis=0)  7.59 us
    slice x4, local copies, waits for them, and re-layouts, shards(): chunks.append(swap(handoff[base:base + size], 'sec', 1))  6.99 us
    ppermute x7, starting transfers between devices, swap(): lax.ppermute(value, axis, [(i, i ^ bit) for i in range(lax.axis_size(axis...  6.89 us
  transfers between devices with their start and end apart: 7, of which 4 were waited for; matrix products, arithmetic and copies ran while one was open for 6% of the time, Pallas kernels for 16%

profile of v2, /device:TPU:0, one launch (start us, length us, event | category | flops | bytes accessed | tf_op | source)
XLA Modules:
  0.0 67.6 jit_solution(7188454864261235948)
XLA Ops:
  0.6 0.0 copy-start.1
  0.6 0.0 copy-start.2
  0.7 0.0 copy-start
  0.7 2.7 %slice_bitcast_fusion = bf16[11,256,256]{2,1,0:T(8,128)(2,1)} fusion(bf16[1,1,17,256,256]{4,3,2,1,0:T(8,128)(2,1)} %param.6), kind=kLoop, calls=%fused_computation | loop fusion | bytes 2883584 | tf_op jit(solution)/shard_map/slice | solution.py:206
  3.4 3.1 %collective-permute-start.3 = (bf16[11,256,256]{2,1,0:T(8,128)(2,1)}, bf16[11,256,256]{2,1,0:T(8,128)(2,1)}, u32[]{:S(2)}, u32[]{:S(2)}) collective-permute-start(bf16[11,256,256]{2,1,0:T(8,128)(2,1)} %slice_bitcast_fusion), channel_id=1, source_target_pairs={{0,4},{4,0},{8,12},{12,8},{1,5},{5,1},{9,13},{13,9},{2,6},{6,2},{1... | collective-permute-start | bytes 4325384 | tf_op jit(solution)/shard_map/ppermute | solution.py:24
  6.4 1.7 %slice_bitcast_fusion.2 = bf16[2,256,256]{2,1,0:T(8,128)(2,1)} fusion(bf16[1,1,17,256,256]{4,3,2,1,0:T(8,128)(2,1)} %param.6), kind=kLoop, calls=%fused_computation.2 | loop fusion | bytes 524288 | tf_op jit(solution)/shard_map/slice | solution.py:206
  8.1 0.0 collective-permute-start
  8.1 1.0 %slice_bitcast_fusion.1 = bf16[3,256,256]{2,1,0:T(8,128)(2,1)S(1)} fusion(bf16[1,1,17,256,256]{4,3,2,1,0:T(8,128)(2,1)} %param.6), kind=kLoop, calls=%fused_computation.1 | loop fusion | bytes 786432 | tf_op jit(solution)/shard_map/slice | solution.py:206
  9.1 2.1 %collective-permute-start.2 = (bf16[3,256,256]{2,1,0:T(8,128)(2,1)S(1)}, bf16[3,256,256]{2,1,0:T(8,128)(2,1)S(1)}, u32[]{:S(2)}, u32[]{:S(2)}) collective-permute-start(bf16[3,256,256]{2,1,0:T(8,128)(2,1)S(1)} %slice_bitcast_fusion.1), channel_id=1, source_target_pairs={{0,4},{4,0},{8,12},{12,8},{1,5},{5,1},{9,13},{13,9},{2,6},{6,2},{1... | collective-permute-start | bytes 1179656 | tf_op jit(solution)/shard_map/ppermute | solution.py:24
  11.2 1.6 %slice_bitcast_fusion.3 = bf16[1,256,256]{2,1,0:T(8,128)(2,1)} fusion(bf16[1,1,17,256,256]{4,3,2,1,0:T(8,128)(2,1)} %param.6), kind=kLoop, calls=%fused_computation.3 | loop fusion | bytes 262144 | tf_op jit(solution)/shard_map/slice | solution.py:206
  12.8 0.0 collective-permute-start.1
  12.8 7.6 %all-gather = bf16[4,1,256,256]{3,2,1,0:T(8,128)(2,1)S(1)} all-gather(bf16[1,1,256,256]{3,2,1,0:T(8,128)(2,1)S(1)} %copy-done.1), channel_id=2, replica_groups=mesh['groups'=2,'sec'=4,'blk'=4] {'blk'}, dimensions={0}, use_global_device_ids=true | all-gather | bytes 655360 | tf_op jit(solution)/shard_map/all_gather | solution.py:212
  20.4 0.0 copy-done.2
  20.4 0.1 pad_add_fusion.table
  20.5 24.2 %collective-permute-done.chunk = bf16[2,256,256]{2,1,0:T(8,128)(2,1)S(1)} collective-permute-done((bf16[2,256,256]{2,1,0:T(8,128)(2,1)}, bf16[2,256,256]{2,1,0:T(8,128)(2,1)S(1)}, u32[]{:S(2)}, u32[]{:S(2)}) %collective-permute-start) | collective-permute-done | bytes 262176 | tf_op jit(solution)/shard_map/ppermute | solution.py:24
  44.7 0.0 copy-done
  44.7 2.3 %shard_map.67 = (bf16[2,17,256,256]{3,2,1,0:T(8,128)(2,1)S(1)}, f32[4,256,256]{2,1,0:T(8,128)S(1)}, f32[4,8,128]{2,1,0:T(8,128)S(1)}, s32[18]{0:T(128)S(1)}, s32[5]{0:T(128)S(1)}) custom-call(s32[19]{0:T(128)S(1)} %pad_add_fusion.table, bf16[4,256,256]{2,1,0:T(8,128)(2,1)S(1)} %bitcast.14, bf16[17,256,256]{2,1,0:T(8,128)(2,1)S(1)} %bitcast.21, ...), custom_call_target="tpu_custom_call" | custom-call | flops 134217728 | tf_op jit(solution)/shard_map/pallas_call | solution.py:36
  47.0 0.0 collective-permute-done.3.chunk
  47.0 3.5 %shard_map.68 = (bf16[2,17,256,256]{3,2,1,0:T(8,128)(2,1)S(1)}, f32[4,256,256]{2,1,0:T(8,128)S(1)}, f32[256,256]{1,0:T(8,128)}, f32[8,128]{1,0:T(8,128)}) custom-call(s32[19]{0:T(128)S(1)} %pad_add_fusion.table, bf16[4,256,256]{2,1,0:T(8,128)(2,1)S(1)} %bitcast.15, ...), custom_call_target="tpu_custom_call", output_to_operand_aliasing={{0}: (3, {}), {1}: (4, {})} | custom-call | flops 738197504 | tf_op jit(solution)/shard_map/pallas_call | solution.py:36
  50.5 2.7 %collective-permute-done.2.chunk = bf16[3,256,256]{2,1,0:T(8,128)(2,1)S(1)} collective-permute-done((bf16[3,256,256]{2,1,0:T(8,128)(2,1)S(1)}, bf16[3,256,256]{2,1,0:T(8,128)(2,1)S(1)}, u32[]{:S(2)}, u32[]{:S(2)}) %collective-permute-start.2) | collective-permute-done | bytes 393248 | tf_op jit(solution)/shard_map/ppermute | solution.py:24
  53.1 1.4 %shard_map.69 = (bf16[2,17,256,256]{3,2,1,0:T(8,128)(2,1)S(1)}, f32[4,256,256]{2,1,0:T(8,128)S(1)}, f32[256,256]{1,0:T(8,128)S(1)}, f32[8,128]{1,0:T(8,128)S(1)}) custom-call(s32[19]{0:T(128)S(1)} %pad_add_fusion.table, bf16[4,256,256]{2,1,0:T(8,128)(2,1)S(1)} %bitcast.16, ...), custom_call_target="tpu_custom_call", output_to_operand_aliasing={{0}: (3, {}), {1}: (4, {})} | custom-call | flops 201326592 | tf_op jit(solution)/shard_map/pallas_call | solution.py:36
  54.5 0.6 collective-permute-done.1.chunk
  55.1 1.2 %shard_map.70 = (bf16[2,17,256,256]{3,2,1,0:T(8,128)(2,1)S(1)}, f32[4,256,256]{2,1,0:T(8,128)S(1)}, bf16[272,256]{1,0:T(8,128)(2,1)S(1)}) custom-call(s32[19]{0:T(128)S(1)} %pad_add_fusion.table, bf16[4,256,256]{2,1,0:T(8,128)(2,1)S(1)} %bitcast.17, ...), custom_call_target="tpu_custom_call", output_to_operand_aliasing={{0}: (3, {}), {1}: (4, {})} | custom-call | flops 67108864 | tf_op jit(solution)/shard_map/pallas_call | solution.py:36
  56.2 1.7 %collective-permute-start.4 = (bf16[272,256]{1,0:T(8,128)(2,1)S(1)}, bf16[272,256]{1,0:T(8,128)(2,1)S(1)}, u32[]{:S(2)}, u32[]{:S(2)}) collective-permute-start(bf16[272,256]{1,0:T(8,128)(2,1)S(1)} %get-tuple-element.36.refs_0_), channel_id=1, source_target_pairs={{0,2},{1,3},{2,0},{3,1},{4,6},{5,7},{6,4},{7,5},{8,10},{9,11},{10,... | collective-permute-start | bytes 417800 | tf_op jit(solution)/shard_map/ppermute | solution.py:24
  58.0 0.0 collective-permute-start.6
  58.0 3.4 %collective-permute-done.4.refs_0_ = bf16[272,256]{1,0:T(8,128)(2,1)S(1)} collective-permute-done((bf16[272,256]{1,0:T(8,128)(2,1)S(1)}, bf16[272,256]{1,0:T(8,128)(2,1)S(1)}, u32[]{:S(2)}, u32[]{:S(2)}) %collective-permute-start.4) | collective-permute-done | bytes 139296 | tf_op jit(solution)/shard_map/ppermute | solution.py:24
  61.4 0.0 collective-permute-start.5
  61.4 0.0 collective-permute-done.6.refs_1_
  61.4 2.3 %shard_map.71 = (f32[256,256]{1,0:T(8,128)S(1)}, f32[2,3,8,128]{3,2,1,0:T(8,128)S(1)}) custom-call(s32[19]{0:T(128)S(1)} %pad_add_fusion.table, s32[18]{0:T(128)S(1)} %get-tuple-element.24.order, s32[5]{0:T(128)S(1)} %get-tuple-element.25.starts, bf16[4,256,256]{2,1,0:T(8,128)(2,1)S(1)} %bitcast.18, bf16[2,17,256,256]{3,2,1,0:T(8,128)(2,1)S(1)} %get-tuple-element.35.env, ...), custom_call_target="tpu_custom_call" | custom-call | flops 570425344 | tf_op jit(solution)/shard_map/pallas_call | solution.py:36
  63.7 1.5 %shard_map.72 = (f32[256,256]{1,0:T(8,128)S(1)}, f32[1,3,8,128]{3,2,1,0:T(8,128)S(1)}) custom-call(s32[19]{0:T(128)S(1)} %pad_add_fusion.table, s32[18]{0:T(128)S(1)} %get-tuple-element.24.order, s32[5]{0:T(128)S(1)} %get-tuple-element.25.starts, bf16[4,256,256]{2,1,0:T(8,128)(2,1)S(1)} %bitcast.19, bf16[2,17,256,256]{3,2,1,0:T(8,128)(2,1)S(1)} %get-tuple-element.35.env, ...), custom_call_target="tpu_custom_call" | custom-call | flops 285212672 | tf_op jit(solution)/shard_map/pallas_call | solution.py:36
  65.3 0.0 collective-permute-done.5.refs_0_
  65.3 2.4 %shard_map.73 = (bf16[256,256]{1,0:T(8,128)(2,1)}, f32[1]{0:T(128)}, f32[1]{0:T(128)}) custom-call(s32[19]{0:T(128)S(1)} %pad_add_fusion.table, s32[18]{0:T(128)S(1)} %get-tuple-element.24.order, s32[5]{0:T(128)S(1)} %get-tuple-element.25.starts, bf16[4,256,256]{2,1,0:T(8,128)(2,1)S(1)} %bitcast.20, bf16[2,17,256,256]{3,2,1,0:T(8,128)(2,1)S(1)} %get-tuple-element.35.env, ...), custom_call_target="tpu_custom_call" | custom-call | flops 285212672 | tf_op jit(solution)/shard_map/pallas_call | solution.py:36
  (1 shorter events, 0.0 us)
Async XLA Ops:
  0.6 12.2 %copy-start.1 = (bf16[1,1,256,256]{3,2,1,0:T(8,128)(2,1)S(1)}, bf16[1,1,256,256]{3,2,1,0:T(8,128)(2,1)}, u32[]{:S(2)}) copy-start(bf16[1,1,256,256]{3,2,1,0:T(8,128)(2,1)} %param.4) | copy-start | bytes 393220
  0.6 19.8 %copy-start.2 = (s32[1,1,17]{2,1,0:T(1,128)S(1)}, s32[1,1,17]{2,1,0:T(1,128)}, u32[]{:S(2)}) copy-start(s32[1,1,17]{2,1,0:T(1,128)} %param.7) | copy-start | bytes 208
  0.7 44.0 %copy-start = (bf16[1,1,17,256,256]{4,3,2,1,0:T(8,128)(2,1)S(1)}, bf16[1,1,17,256,256]{4,3,2,1,0:T(8,128)(2,1)}, u32[]{:S(2)}) copy-start(bf16[1,1,17,256,256]{4,3,2,1,0:T(8,128)(2,1)} %param.5) | copy-start | bytes 6684676
  3.4 43.6 %collective-permute-start.3 = (bf16[11,256,256]{2,1,0:T(8,128)(2,1)}, bf16[11,256,256]{2,1,0:T(8,128)(2,1)}, u32[]{:S(2)}, u32[]{:S(2)}) collective-permute-start(bf16[11,256,256]{2,1,0:T(8,128)(2,1)} %slice_bitcast_fusion), channel_id=1, source_target_pairs={{0,4},{4,0},{8,12},{12,8},{1,5},{5,1},{9,13},{13,9},{2,6},{6,2},{1... | collective-permute-start | bytes 4325384 | tf_op jit(solution)/shard_map/ppermute | solution.py:24
  8.1 36.6 %collective-permute-start = (bf16[2,256,256]{2,1,0:T(8,128)(2,1)}, bf16[2,256,256]{2,1,0:T(8,128)(2,1)S(1)}, u32[]{:S(2)}, u32[]{:S(2)}) collective-permute-start(bf16[2,256,256]{2,1,0:T(8,128)(2,1)} %slice_bitcast_fusion.2), channel_id=1, source_target_pairs={{0,4},{4,0},{8,12},{12,8},{1,5},{5,1},{9,13},{13,9},{2,6},{6,2},{1... | collective-permute-start | bytes 786440 | tf_op jit(solution)/shard_map/ppermute | solution.py:24
  9.1 44.0 %collective-permute-start.2 = (bf16[3,256,256]{2,1,0:T(8,128)(2,1)S(1)}, bf16[3,256,256]{2,1,0:T(8,128)(2,1)S(1)}, u32[]{:S(2)}, u32[]{:S(2)}) collective-permute-start(bf16[3,256,256]{2,1,0:T(8,128)(2,1)S(1)} %slice_bitcast_fusion.1), channel_id=1, source_target_pairs={{0,4},{4,0},{8,12},{12,8},{1,5},{5,1},{9,13},{13,9},{2,6},{6,2},{1... | collective-permute-start | bytes 1179656 | tf_op jit(solution)/shard_map/ppermute | solution.py:24
  12.8 42.3 %collective-permute-start.1 = (bf16[1,256,256]{2,1,0:T(8,128)(2,1)}, bf16[1,256,256]{2,1,0:T(8,128)(2,1)S(1)}, u32[]{:S(2)}, u32[]{:S(2)}) collective-permute-start(bf16[1,256,256]{2,1,0:T(8,128)(2,1)} %slice_bitcast_fusion.3), channel_id=1, source_target_pairs={{0,4},{4,0},{8,12},{12,8},{1,5},{5,1},{9,13},{13,9},{2,6},{6,2},{1... | collective-permute-start | bytes 393224 | tf_op jit(solution)/shard_map/ppermute | solution.py:24
  56.2 5.1 %collective-permute-start.4 = (bf16[272,256]{1,0:T(8,128)(2,1)S(1)}, bf16[272,256]{1,0:T(8,128)(2,1)S(1)}, u32[]{:S(2)}, u32[]{:S(2)}) collective-permute-start(bf16[272,256]{1,0:T(8,128)(2,1)S(1)} %get-tuple-element.36.refs_0_), channel_id=1, source_target_pairs={{0,2},{1,3},{2,0},{3,1},{4,6},{5,7},{6,4},{7,5},{8,10},{9,11},{10,... | collective-permute-start | bytes 417800 | tf_op jit(solution)/shard_map/ppermute | solution.py:24
  58.0 3.4 %collective-permute-start.6 = (bf16[272,256]{1,0:T(8,128)(2,1)S(1)}, bf16[272,256]{1,0:T(8,128)(2,1)S(1)}, u32[]{:S(2)}, u32[]{:S(2)}) collective-permute-start(bf16[272,256]{1,0:T(8,128)(2,1)S(1)} %get-tuple-element.36.refs_0_), channel_id=1, source_target_pairs={{0,1},{1,0},{2,3},{3,2},{4,5},{5,4},{6,7},{7,6},{8,9},{9,8},{10,11... | collective-permute-start | bytes 417800 | tf_op jit(solution)/shard_map/ppermute | solution.py:24
  61.4 3.9 %collective-permute-start.5 = (bf16[272,256]{1,0:T(8,128)(2,1)S(1)}, bf16[272,256]{1,0:T(8,128)(2,1)S(1)}, u32[]{:S(2)}, u32[]{:S(2)}) collective-permute-start(bf16[272,256]{1,0:T(8,128)(2,1)S(1)} %collective-permute-done.4.refs_0_), channel_id=1, source_target_pairs={{0,1},{1,0},{2,3},{3,2},{4,5},{5,4},{6,7},{7,6},{8,9},{9,8},{10,11... | collective-permute-start | bytes 417800 | tf_op jit(solution)/shard_map/ppermute | solution.py:24

commit v3 on v2

--- a/solution.py
+++ b/solution.py
@@ -52,12 +52,20 @@
     return source, dot(env[parity, c], inner)
 
 
-def opening_kernel(table, psi, own, chunk, env, parts, mass, order, starts, sem):
+def cut_kernel(whole, piece, sem):
+    copy = pltpu.make_async_copy(whole.at[pl.ds(0, piece.shape[0])], piece, sem)
+    copy.start()
+    copy.wait()
+
+
+def opening_kernel(table, psi, own, chunk, env, parts, mass, order, starts, kept, sem):
     copy = pltpu.make_async_copy(own, env.at[0], sem)
     copy.start()
     channels = own.shape[0]
     width = psi.shape[0]
     me = table[1]
+    for k in range(table.shape[0]):
+        kept[k] = table[k]
     for k in range(chunk.shape[0]):
         env[1, k] = chunk[k]
     parts[...] = jnp.zeros_like(parts)
@@ -118,59 +126,73 @@
     packed[rows:] = tail.astype(bf16)
 
 
-def second_kernel(low, high, more, width, table, order, starts, psi, env, *refs):
+def gathered(table, order, psi_rows, env, blocks, held, low, begin, end):
+    parity, me = table[0], table[1]
+    lefts, inners = [], []
+    for k in range(GROUP):
+        valid = begin + k < end
+        c = order[jnp.where(valid, begin + k, 0)]
+        if len(blocks) > 1:
+            vector = held[jnp.where(valid, (table[2 + c] ^ me) - low, 0)]
+        else:
+            vector = blocks[0][:psi_rows]
+        inner = dot(vector, env[1 - parity, c])
+        inners.append(jnp.where(valid, inner, 0.0).astype(bf16))
+        lefts.append(env[parity, c])
+    return dot(jnp.concatenate(lefts, axis=1), jnp.concatenate(inners, axis=0))
+
+
+def own_sums(block, psi):
+    rows = psi.shape[0]
+    bits = block[rows:].astype(f32)
+    share = bits[0:1, 0:1] + bits[1:2, 0:1] + bits[2:3, 0:1]
+    value = block[:rows].astype(f32)
+    return share, total_of(value * value), total_of(value * psi[...].astype(f32))
+
+
+def second_kernel(low, high, table, order, starts, psi, env, *refs):
     count = high - low
     blocks, refs = refs[:count], refs[count:]
     if low:
         before, refs = refs[0], refs[1:]
-    if high == width:
-        (mass, parts), refs = refs[:2], refs[2:]
-        stats_in, refs = refs[:more], refs[more:]
-        applied, alpha_out, scale_out, summed, held = refs
-    else:
-        summed, stats, held = refs
-    parity, me = table[0], table[1]
+    summed, stats, held = refs
+    me = table[1]
     rows, columns = psi.shape[1:]
-
-    for k in range(count):
-        held[k] = blocks[k][:rows]
-
+    if count > 1:
+        for k in range(count):
+            held[k] = blocks[k][:rows]
     summed[...] = before[...] if low else jnp.zeros((rows, columns), f32)
     begin, end = starts[low], starts[high]
 
     def step(g, carry):
-        total = None
-        for k in range(GROUP):
-            place = begin + g * GROUP + k
-            valid = place < end
-            c = order[jnp.where(valid, place, 0)]
-            m = jnp.where(valid, (table[2 + c] ^ me) - low, 0)
-            inner = jnp.where(valid, dot(held[m], env[1 - parity, c]), 0.0).astype(bf16)
-            product = dot(env[parity, c], inner)
-            total = product if total is None else total + product
-        summed[...] += total
+        summed[...] += gathered(table, order, rows, env, blocks, held, low, begin + g * GROUP, end)
         return carry
 
     lax.fori_loop(0, (end - begin + GROUP - 1) // GROUP, step, 0)
-
-    mine = []
     for k in range(count):
-        bits = blocks[k][rows:].astype(f32)
-        share = bits[0:1, 0:1] + bits[1:2, 0:1] + bits[2:3, 0:1]
-        value = held[k].astype(f32)
-        cross = total_of(value * psi[me ^ (low + k)].astype(f32))
-        mine.append((share, total_of(value * value), cross))
-    if high < width:
-        for k in range(count):
-            for j in range(3):
-                stats[k, j] = jnp.broadcast_to(mine[k][j], stats.shape[2:])
-        return
+        for j, value in enumerate(own_sums(blocks[k], psi.at[me ^ (low + k)])):
+            stats[k, j] = jnp.broadcast_to(value, stats.shape[2:])
+
+
+def final_kernel(low, more, table, order, starts, psi, env, block, before, mass, parts, *refs):
+    stats_in, refs = refs[:more], refs[more:]
+    applied, alpha_out, scale_out, summed, ready, alpha_held, scale_held, sem = refs
+    me = table[1]
+    width, rows, columns = parts.shape
+    begin, end = starts[low], starts[width]
+    summed[...] = before[...]
+
+    def step(g, carry):
+        summed[...] += gathered(table, order, rows, env, [block], None, low, begin + g * GROUP, end)
+        return carry
+
+    lax.fori_loop(1, (end - begin + GROUP - 1) // GROUP, step, 0)
 
     triples = []
     for ref in stats_in:
         for k in range(ref.shape[0]):
             triples.append(tuple(ref[k, j][:1, :1] for j in range(3)))
-    triples += mine
+    triples.append(own_sums(block, psi.at[me ^ low]))
     along = jnp.zeros((1, 1), f32)
     whole = jnp.zeros((1, 1), f32)
     for m in range(width):
@@ -186,9 +208,20 @@
         power += square + 2.0 * delta * cross + delta * delta * mass[me ^ m][:1, :1]
         total += delta * parts[me ^ m]
     scale = jnp.sqrt(power / (width * rows * columns) + 1e-06)
-    applied[...] = (total / scale).astype(bf16)
-    alpha_out[0] = alpha[0, 0]
-    scale_out[0] = scale[0, 0]
+    alpha_held[0] = alpha[0, 0]
+    scale_held[0] = scale[0, 0]
+    copies = [
+        pltpu.make_async_copy(alpha_held, alpha_out, sem.at[0]),
+        pltpu.make_async_copy(scale_held, scale_out, sem.at[1]),
+        pltpu.make_async_copy(ready, applied, sem.at[2]),
+    ]
+    copies[0].start()
+    copies[1].start()
+    total += gathered(table, order, rows, env, [block], None, low, begin, end)
+    ready[...] = (total / scale).astype(bf16)
+    copies[2].start()
+    for copy in copies:
+        copy.wait()
 
 
 def chunk_sizes(channels):
@@ -202,8 +235,19 @@
     work = 4 * block[0] ** 3
     sizes = chunk_sizes(channels)
     chunks, bases, base = [], [], 0
-    for size in sizes:
-        chunks.append(swap(handoff[base : base + size], "sec", 1))
+    for k, size in enumerate(sizes):
+        if k == 0:
+            (piece,) = call(
+                cut_kernel,
+                [HBM],
+                [(VMEM, pltpu.VMEM((size,) + block, bf16))],
+                (pltpu.with_memory_space_constraint(handoff, pltpu.HBM),),
+                0,
+                scratch=[pltpu.SemaphoreType.DMA],
+            )
+        else:
+            piece = handoff[base : base + size]
+        chunks.append(swap(piece, "sec", 1))
         bases.append(base)
         base += size
     table = jnp.concatenate(
@@ -214,17 +258,18 @@
     env_shape = (VMEM, pltpu.VMEM((2, channels) + block, bf16))
     parts_shape = (VMEM, pltpu.VMEM((width,) + block, f32))
     tile = (8, 128)
-    env, parts, mass, order, starts = call(
+    env, parts, mass, order, starts, table = call(
         opening_kernel,
         [SMEM, VMEM, HBM, VMEM],
         [
             env_shape,
             parts_shape,
             (VMEM, pltpu.VMEM((width,) + tile, f32)),
-            (SMEM, jax.ShapeDtypeStruct((channels + 1,), jnp.int32)),
-            (SMEM, jax.ShapeDtypeStruct((width + 1,), jnp.int32)),
+            (SMEM, pltpu.SMEM((channels + 1,), jnp.int32)),
+            (SMEM, pltpu.SMEM((width + 1,), jnp.int32)),
+            (SMEM, pltpu.SMEM(table.shape, jnp.int32)),
         ],
-        (table, psis, own, chunks[0]),
+        (table, psis, pltpu.with_memory_space_constraint(own, pltpu.HBM), chunks[0]),
         work * sizes[0],
         scratch=[pltpu.SemaphoreType.DMA],
     )
@@ -253,43 +298,41 @@
             blocks[m | bit] = swap(blocks[m], "blk", bit)
         bit //= 2
 
-    cuts = sorted({0, min(2, width - 1), width - 1, width})
+    cuts = sorted({0, min(2, width - 1), width - 1})
+    shared = [table, order, starts, psis, env]
+    shared_specs = [SMEM, SMEM, SMEM, VMEM, VMEM]
     summed, stats = None, []
     for low, high in zip(cuts[:-1], cuts[1:]):
         count = high - low
-        last = high == width
-        args = [table, order, starts, psis, env] + [blocks[m] for m in range(low, high)]
-        specs = [SMEM, SMEM, SMEM, VMEM, VMEM] + [VMEM] * count
-        if low:
-            args.append(summed)
-            specs.append(VMEM)
-        scratch = [pltpu.VMEM((count,) + block, bf16)]
-        if last:
-            args += [mass, parts] + stats
-            specs += [VMEM] * (2 + len(stats))
-            outs = [
-                (VMEM, jax.ShapeDtypeStruct(block, bf16)),
-                (SMEM, jax.ShapeDtypeStruct((1,), f32)),
-                (SMEM, jax.ShapeDtypeStruct((1,), f32)),
-            ]
-            scratch = [pltpu.VMEM(block, f32)] + scratch
-        else:
-            outs = [
-                (VMEM, pltpu.VMEM(block, f32)),
-                (VMEM, pltpu.VMEM((count, 3) + tile, f32)),
-            ]
-        result = call(
-            functools.partial(second_kernel, low, high, len(stats), width),
-            specs,
-            outs,
+        args = shared + [blocks[m] for m in range(low, high)] + ([summed] if low else [])
+        summed, stat = call(
+            functools.partial(second_kernel, low, high),
+            shared_specs + [VMEM] * (len(args) - len(shared)),
+            [(VMEM, pltpu.VMEM(block, f32)), (VMEM, pltpu.VMEM((count, 3) + tile, f32))],
             tuple(args),
             work * channels * count // width,
-            scratch=scratch,
+            scratch=[pltpu.VMEM((count,) + block, bf16)],
         )
-        if not last:
-            summed = result[0]
-            stats.append(result[1])
-    applied, alpha, scale = result
+        stats.append(stat)
+    args = shared + [blocks[width - 1], summed, mass, parts] + stats
+    applied, alpha, scale = call(
+        functools.partial(final_kernel, width - 1, len(stats)),
+        shared_specs + [VMEM] * (len(args) - len(shared)),
+        [
+            (HBM, jax.ShapeDtypeStruct(block, bf16)),
+            (HBM, jax.ShapeDtypeStruct((1,), f32)),
+            (HBM, jax.ShapeDtypeStruct((1,), f32)),
+        ],
+        tuple(args),
+        work * channels // width,
+        scratch=[
+            pltpu.VMEM(block, f32),
+            pltpu.VMEM(block, bf16),
+            pltpu.SMEM((1,), f32),
+            pltpu.SMEM((1,), f32),
+            pltpu.SemaphoreType.DMA((3,)),
+        ],
+    )
     return applied[None, None], alpha, scale
 
 

time: 67.9 us -> 65 us (0.957)
  Pallas kernels: 14.5 us -> 11.1 us
  waiting for transfers between devices: 30.8 us -> 33.7 us
  local copies, waits for them, and re-layouts: 7.01 us -> 4.51 us
    pallas_call x7 -> x8, Pallas kernels: 14.5 us -> 11.1 us  [call(): pl.pallas_call(kernel, in_specs=ins, out_specs=[spec for spec, _ in outs]...]
    ppermute x7, waiting for transfers between devices: 30.8 us -> 33.7 us  [swap(): lax.ppermute(value, axis, [(i, i ^ bit) for i in range(lax.axis_size(axis...]
    slice x4 -> x3, local copies, waits for them, and re-layouts: 6.99 us -> 4.5 us  [shards(): piece = handoff[base:base + size]]
  transfers between devices with their start and end apart: 7 -> 7, of which waited for: 4 -> 4; matrix products, arithmetic and copies ran while one was open for 6% -> 3% of each run, Pallas kernels for 16% -> 14%
where the time goes in v3:
time: 65 us; the launch traced here: 64.7 us
  waiting for transfers between devices  33.7 us (52%)
  Pallas kernels  11.1 us (17%)
  blocking collectives  7.57 us (12%)
  starting transfers between devices  7.04 us (11%)
  local copies, waits for them, and re-layouts  4.51 us (7%)
  between operations  0.71 us (1%)
    ppermute x7, waiting for transfers between devices, swap(): lax.ppermute(value, axis, [(i, i ^ bit) for i in range(lax.axis_size(axis...  33.7 us
    pallas_call x8, Pallas kernels, call(): pl.pallas_call(kernel, in_specs=ins, out_specs=[spec for spec, _ in outs]...  11.1 us
    all_gather x1, blocking collectives, shards(): psis = lax.all_gather(psi[0, 0], 'blk', axis=0)  7.57 us
    ppermute x7, starting transfers between devices, swap(): lax.ppermute(value, axis, [(i, i ^ bit) for i in range(lax.axis_size(axis...  7.04 us
    slice x3, local copies, waits for them, and re-layouts, shards(): piece = handoff[base:base + size]  4.5 us
  transfers between devices with their start and end apart: 7, of which 4 were waited for; matrix products, arithmetic and copies ran while one was open for 3% of the time, Pallas kernels for 14%

profile of v3, /device:TPU:0, one launch (start us, length us, event | category | flops | bytes accessed | tf_op | source)
XLA Modules:
  0.0 64.7 jit_solution(7257230439586960392)
XLA Ops:
  0.6 2.6 %slice_bitcast_fusion = bf16[11,256,256]{2,1,0:T(8,128)(2,1)} fusion(bf16[1,1,17,256,256]{4,3,2,1,0:T(8,128)(2,1)} %param.6), kind=kLoop, calls=%fused_computation | loop fusion | bytes 2883584 | tf_op jit(solution)/shard_map/slice | solution.py:249
  3.2 0.0 copy-start
  3.2 0.0 copy-start.1
  3.2 3.1 %collective-permute-start.3 = (bf16[11,256,256]{2,1,0:T(8,128)(2,1)}, bf16[11,256,256]{2,1,0:T(8,128)(2,1)S(1)}, u32[]{:S(2)}, u32[]{:S(2)}) collective-permute-start(bf16[11,256,256]{2,1,0:T(8,128)(2,1)} %slice_bitcast_fusion), channel_id=1, source_target_pairs={{0,4},{4,0},{8,12},{12,8},{1,5},{5,1},{9,13},{13,9},{2,6},{6,2},{1... | collective-permute-start | bytes 4325384 | tf_op jit(solution)/shard_map/ppermute | solution.py:24
  6.3 1.0 %shard_map.67 = bf16[2,256,256]{2,1,0:T(8,128)(2,1)S(1)} custom-call(bf16[17,256,256]{2,1,0:T(8,128)(2,1)} %bitcast.20), custom_call_target="tpu_custom_call" | custom-call | tf_op jit(solution)/shard_map/pallas_call | solution.py:36
  7.2 0.1 collective-permute-start
  7.3 1.0 %slice_bitcast_fusion.1 = bf16[3,256,256]{2,1,0:T(8,128)(2,1)S(1)} fusion(bf16[1,1,17,256,256]{4,3,2,1,0:T(8,128)(2,1)} %param.6), kind=kLoop, calls=%fused_computation.1 | loop fusion | bytes 786432 | tf_op jit(solution)/shard_map/slice | solution.py:249
  8.3 2.1 %collective-permute-start.2 = (bf16[3,256,256]{2,1,0:T(8,128)(2,1)S(1)}, bf16[3,256,256]{2,1,0:T(8,128)(2,1)S(1)}, u32[]{:S(2)}, u32[]{:S(2)}) collective-permute-start(bf16[3,256,256]{2,1,0:T(8,128)(2,1)S(1)} %slice_bitcast_fusion.1), channel_id=1, source_target_pairs={{0,4},{4,0},{8,12},{12,8},{1,5},{5,1},{9,13},{13,9},{2,6},{6,2},{1... | collective-permute-start | bytes 1179656 | tf_op jit(solution)/shard_map/ppermute | solution.py:24
  10.4 0.9 %slice_bitcast_fusion.2 = bf16[1,256,256]{2,1,0:T(8,128)(2,1)S(1)} fusion(bf16[1,1,17,256,256]{4,3,2,1,0:T(8,128)(2,1)} %param.6), kind=kLoop, calls=%fused_computation.2 | loop fusion | bytes 262144 | tf_op jit(solution)/shard_map/slice | solution.py:249
  11.3 0.1 collective-permute-start.1
  11.4 0.0 copy-done
  11.4 7.6 %all-gather = bf16[4,1,256,256]{3,2,1,0:T(8,128)(2,1)S(1)} all-gather(bf16[1,1,256,256]{3,2,1,0:T(8,128)(2,1)S(1)} %copy-done), channel_id=2, replica_groups=mesh['groups'=2,'sec'=4,'blk'=4] {'blk'}, dimensions={0}, use_global_device_ids=true | all-gather | bytes 655360 | tf_op jit(solution)/shard_map/all_gather | solution.py:256
  19.0 0.0 copy-done.1
  19.0 0.1 pad_add_fusion.table
  19.1 25.4 %collective-permute-done.chunk = bf16[2,256,256]{2,1,0:T(8,128)(2,1)S(1)} collective-permute-done((bf16[2,256,256]{2,1,0:T(8,128)(2,1)S(1)}, bf16[2,256,256]{2,1,0:T(8,128)(2,1)S(1)}, u32[]{:S(2)}, u32[]{:S(2)}) %collective-permute-start) | collective-permute-done | bytes 262176 | tf_op jit(solution)/shard_map/ppermute | solution.py:24
  44.5 2.7 %shard_map.68 = (bf16[2,17,256,256]{3,2,1,0:T(8,128)(2,1)S(1)}, f32[4,256,256]{2,1,0:T(8,128)S(1)}, f32[4,8,128]{2,1,0:T(8,128)S(1)}, s32[18]{0:T(128)S(4)}, s32[5]{0:T(128)S(4)}, /*index=5*/s32[19]{0:T(128)S(4)}) custom-call(s32[19]{0:T(128)S(1)} %pad_add_fusion.table, bf16[4,256,256]{2,1,0:T(8,128)(2,1)S(1)} %bitcast.13, bf16[17,256,256]{2,1,0:T(8,128)(2,1)} %bitcast.21, ...), custom_call_target="tpu_custom_call" | custom-call | flops 134217728 | tf_op jit(solution)/shard_map/pallas_call | solution.py:36
  47.2 0.0 collective-permute-done.3.chunk
  47.2 2.0 %shard_map.69 = (bf16[2,17,256,256]{3,2,1,0:T(8,128)(2,1)S(1)}, f32[4,256,256]{2,1,0:T(8,128)S(1)}, f32[256,256]{1,0:T(8,128)}, f32[8,128]{1,0:T(8,128)}) custom-call(s32[19]{0:T(128)S(4)} %get-tuple-element.25.table, bf16[4,256,256]{2,1,0:T(8,128)(2,1)S(1)} %bitcast.14, ...), custom_call_target="tpu_custom_call", output_to_operand_aliasing={{0}: (3, {}), {1}: (4, {})} | custom-call | flops 738197504 | tf_op jit(solution)/shard_map/pallas_call | solution.py:36
  49.2 3.7 %collective-permute-done.2.chunk = bf16[3,256,256]{2,1,0:T(8,128)(2,1)S(1)} collective-permute-done((bf16[3,256,256]{2,1,0:T(8,128)(2,1)S(1)}, bf16[3,256,256]{2,1,0:T(8,128)(2,1)S(1)}, u32[]{:S(2)}, u32[]{:S(2)}) %collective-permute-start.2) | collective-permute-done | bytes 393248 | tf_op jit(solution)/shard_map/ppermute | solution.py:24
  52.9 0.8 %shard_map.70 = (bf16[2,17,256,256]{3,2,1,0:T(8,128)(2,1)S(1)}, f32[4,256,256]{2,1,0:T(8,128)S(1)}, f32[256,256]{1,0:T(8,128)S(1)}, f32[8,128]{1,0:T(8,128)S(1)}) custom-call(s32[19]{0:T(128)S(4)} %get-tuple-element.25.table, bf16[4,256,256]{2,1,0:T(8,128)(2,1)S(1)} %bitcast.15, ...), custom_call_target="tpu_custom_call", output_to_operand_aliasing={{0}: (3, {}), {1}: (4, {})} | custom-call | flops 201326592 | tf_op jit(solution)/shard_map/pallas_call | solution.py:36
  53.8 1.1 %collective-permute-done.1.chunk = bf16[1,256,256]{2,1,0:T(8,128)(2,1)S(1)} collective-permute-done((bf16[1,256,256]{2,1,0:T(8,128)(2,1)S(1)}, bf16[1,256,256]{2,1,0:T(8,128)(2,1)S(1)}, u32[]{:S(2)}, u32[]{:S(2)}) %collective-permute-start.1) | collective-permute-done | bytes 131104 | tf_op jit(solution)/shard_map/ppermute | solution.py:24
  54.9 0.6 shard_map.71
  55.5 1.7 %collective-permute-start.4 = (bf16[272,256]{1,0:T(8,128)(2,1)S(1)}, bf16[272,256]{1,0:T(8,128)(2,1)S(1)}, u32[]{:S(2)}, u32[]{:S(2)}) collective-permute-start(bf16[272,256]{1,0:T(8,128)(2,1)S(1)} %get-tuple-element.38.refs_0_), channel_id=1, source_target_pairs={{0,2},{1,3},{2,0},{3,1},{4,6},{5,7},{6,4},{7,5},{8,10},{9,11},{10,... | collective-permute-start | bytes 417800 | tf_op jit(solution)/shard_map/ppermute | solution.py:24
  57.2 0.0 collective-permute-start.6
  57.2 3.4 %collective-permute-done.4.refs_0_ = bf16[272,256]{1,0:T(8,128)(2,1)S(1)} collective-permute-done((bf16[272,256]{1,0:T(8,128)(2,1)S(1)}, bf16[272,256]{1,0:T(8,128)(2,1)S(1)}, u32[]{:S(2)}, u32[]{:S(2)}) %collective-permute-start.4) | collective-permute-done | bytes 139296 | tf_op jit(solution)/shard_map/ppermute | solution.py:24
  60.6 0.0 collective-permute-start.5
  60.6 0.0 collective-permute-done.6.refs_1_
  60.6 1.7 %shard_map.72 = (f32[256,256]{1,0:T(8,128)S(1)}, f32[2,3,8,128]{3,2,1,0:T(8,128)S(1)}) custom-call(s32[19]{0:T(128)S(4)} %get-tuple-element.25.table, s32[18]{0:T(128)S(4)} %get-tuple-element.26.order, s32[5]{0:T(128)S(4)} %get-tuple-element.27.starts, bf16[4,256,256]{2,1,0:T(8,128)(2,1)S(1)} %bitcast.17, ...), custom_call_target="tpu_custom_call" | custom-call | flops 570425344 | tf_op jit(solution)/shard_map/pallas_call | solution.py:36
  62.3 0.9 %shard_map.73 = (f32[256,256]{1,0:T(8,128)S(1)}, f32[1,3,8,128]{3,2,1,0:T(8,128)S(1)}) custom-call(s32[19]{0:T(128)S(4)} %get-tuple-element.25.table, s32[18]{0:T(128)S(4)} %get-tuple-element.26.order, s32[5]{0:T(128)S(4)} %get-tuple-element.27.starts, bf16[4,256,256]{2,1,0:T(8,128)(2,1)S(1)} %bitcast.18, ...), custom_call_target="tpu_custom_call" | custom-call | flops 285212672 | tf_op jit(solution)/shard_map/pallas_call | solution.py:36
  63.2 0.0 collective-permute-done.5.block
  63.3 1.4 %shard_map.74 = (bf16[256,256]{1,0:T(8,128)(2,1)}, f32[1]{0:T(128)}, f32[1]{0:T(128)}) custom-call(s32[19]{0:T(128)S(4)} %get-tuple-element.25.table, s32[18]{0:T(128)S(4)} %get-tuple-element.26.order, s32[5]{0:T(128)S(4)} %get-tuple-element.27.starts, bf16[4,256,256]{2,1,0:T(8,128)(2,1)S(1)} %bitcast.19, ...), custom_call_target="tpu_custom_call" | custom-call | flops 285212672 | tf_op jit(solution)/shard_map/pallas_call | solution.py:36
Async XLA Ops:
  3.2 8.2 %copy-start = (bf16[1,1,256,256]{3,2,1,0:T(8,128)(2,1)S(1)}, bf16[1,1,256,256]{3,2,1,0:T(8,128)(2,1)}, u32[]{:S(2)}) copy-start(bf16[1,1,256,256]{3,2,1,0:T(8,128)(2,1)} %param.4) | copy-start | bytes 393220
  3.2 15.8 %copy-start.1 = (s32[1,1,17]{2,1,0:T(1,128)S(1)}, s32[1,1,17]{2,1,0:T(1,128)}, u32[]{:S(2)}) copy-start(s32[1,1,17]{2,1,0:T(1,128)} %param.7) | copy-start | bytes 208
  3.2 44.0 %collective-permute-start.3 = (bf16[11,256,256]{2,1,0:T(8,128)(2,1)}, bf16[11,256,256]{2,1,0:T(8,128)(2,1)S(1)}, u32[]{:S(2)}, u32[]{:S(2)}) collective-permute-start(bf16[11,256,256]{2,1,0:T(8,128)(2,1)} %slice_bitcast_fusion), channel_id=1, source_target_pairs={{0,4},{4,0},{8,12},{12,8},{1,5},{5,1},{9,13},{13,9},{2,6},{6,2},{1... | collective-permute-start | bytes 4325384 | tf_op jit(solution)/shard_map/ppermute | solution.py:24
  7.2 37.3 %collective-permute-start = (bf16[2,256,256]{2,1,0:T(8,128)(2,1)S(1)}, bf16[2,256,256]{2,1,0:T(8,128)(2,1)S(1)}, u32[]{:S(2)}, u32[]{:S(2)}) collective-permute-start(bf16[2,256,256]{2,1,0:T(8,128)(2,1)S(1)} %shard_map.67), channel_id=1, source_target_pairs={{0,4},{4,0},{8,12},{12,8},{1,5},{5,1},{9,13},{13,9},{2,6},{6,2},{1... | collective-permute-start | bytes 786440 | tf_op jit(solution)/shard_map/ppermute | solution.py:24
  8.3 44.6 %collective-permute-start.2 = (bf16[3,256,256]{2,1,0:T(8,128)(2,1)S(1)}, bf16[3,256,256]{2,1,0:T(8,128)(2,1)S(1)}, u32[]{:S(2)}, u32[]{:S(2)}) collective-permute-start(bf16[3,256,256]{2,1,0:T(8,128)(2,1)S(1)} %slice_bitcast_fusion.1), channel_id=1, source_target_pairs={{0,4},{4,0},{8,12},{12,8},{1,5},{5,1},{9,13},{13,9},{2,6},{6,2},{1... | collective-permute-start | bytes 1179656 | tf_op jit(solution)/shard_map/ppermute | solution.py:24
  11.3 43.6 %collective-permute-start.1 = (bf16[1,256,256]{2,1,0:T(8,128)(2,1)S(1)}, bf16[1,256,256]{2,1,0:T(8,128)(2,1)S(1)}, u32[]{:S(2)}, u32[]{:S(2)}) collective-permute-start(bf16[1,256,256]{2,1,0:T(8,128)(2,1)S(1)} %slice_bitcast_fusion.2), channel_id=1, source_target_pairs={{0,4},{4,0},{8,12},{12,8},{1,5},{5,1},{9,13},{13,9},{2,6},{6,2},{1... | collective-permute-start | bytes 393224 | tf_op jit(solution)/shard_map/ppermute | solution.py:24
  55.5 5.1 %collective-permute-start.4 = (bf16[272,256]{1,0:T(8,128)(2,1)S(1)}, bf16[272,256]{1,0:T(8,128)(2,1)S(1)}, u32[]{:S(2)}, u32[]{:S(2)}) collective-permute-start(bf16[272,256]{1,0:T(8,128)(2,1)S(1)} %get-tuple-element.38.refs_0_), channel_id=1, source_target_pairs={{0,2},{1,3},{2,0},{3,1},{4,6},{5,7},{6,4},{7,5},{8,10},{9,11},{10,... | collective-permute-start | bytes 417800 | tf_op jit(solution)/shard_map/ppermute | solution.py:24
  57.2 3.4 %collective-permute-start.6 = (bf16[272,256]{1,0:T(8,128)(2,1)S(1)}, bf16[272,256]{1,0:T(8,128)(2,1)S(1)}, u32[]{:S(2)}, u32[]{:S(2)}) collective-permute-start(bf16[272,256]{1,0:T(8,128)(2,1)S(1)} %get-tuple-element.38.refs_0_), channel_id=1, source_target_pairs={{0,1},{1,0},{2,3},{3,2},{4,5},{5,4},{6,7},{7,6},{8,9},{9,8},{10,11... | collective-permute-start | bytes 417800 | tf_op jit(solution)/shard_map/ppermute | solution.py:24
  60.6 2.6 %collective-permute-start.5 = (bf16[272,256]{1,0:T(8,128)(2,1)S(1)}, bf16[272,256]{1,0:T(8,128)(2,1)S(1)}, u32[]{:S(2)}, u32[]{:S(2)}) collective-permute-start(bf16[272,256]{1,0:T(8,128)(2,1)S(1)} %collective-permute-done.4.refs_0_), channel_id=1, source_target_pairs={{0,1},{1,0},{2,3},{3,2},{4,5},{5,4},{6,7},{7,6},{8,9},{9,8},{10,11... | collective-permute-start | bytes 417800 | tf_op jit(solution)/shard_map/ppermute | solution.py:24
